TPU v7x, 32 devices: a whole 2x2x4 slice. The times are simulated.
32 devices in a mesh: sub: 4 (over x, core), lat: 2 (over y), lon: 4 (over z).
Axes of the slice: x: 2, y: 2, z: 4, core: 2. Of those that a mesh axis runs over, the one named last changes fastest.
Arguments:
- segment_launch_values: float32 [4, 3, 1024, 1024], P('sub', None, 'lat', 'lon'), may hold values from -1.8 to 1.8
- initial_backdrop: float32 [3, 1024, 1024], P(None, 'lat', 'lon'), may hold values from -1.8 to 1.8
- spectral_inverse_variances: float32 [3, 513], replicated, may hold values from 0.3 to 3
Outputs:
- weighted_defects: float32 [4, 3, 1024, 1024], P('sub', None, 'lat', 'lon')
All inputs are finite; a program needn't handle non-finite values.
Results may differ from a plain program's by a relative error of at most 0.00017.
Values sent between devices are 32-bit elements; how exact they have to be, the bound alone decides.
A program may use at most 64 MiB of HBM per device.

v0:
```python
import jax
import jax.numpy as jnp
from jax import lax
from jax.sharding import PartitionSpec as P

NLON = 1024
STEPS = 3


time_step = 0.5
coriolis_peak = 0.4


def padded_2(block, sides, width):
    for axis, dim in sides:
        count = lax.axis_size(axis)
        forward = [(i, i + 1) for i in range(count - 1)]
        forward.append((count - 1, 0))
        backward = [(target, source) for source, target in forward]
        low = lax.ppermute(
            lax.slice_in_dim(block, block.shape[dim] - width, None, axis=dim), axis, forward
        )
        high = lax.ppermute(lax.slice_in_dim(block, 0, width, axis=dim), axis, backward)
        block = jnp.concatenate([low, block, high], axis=dim)
    return block


def from_behind(value, axis, steps):
    count = lax.axis_size(axis)
    first, last = (max(0, -steps), min(count, count - steps))
    return lax.ppermute(value, axis, [(source, source + steps) for source in range(first, last)])


def latitude_tendencies(total_rows, first_row, count):
    index = (first_row + jnp.arange(count)).astype(jnp.float32)
    return (coriolis_peak * jnp.sin(2.0 * jnp.pi * (index + 0.5) / total_rows))[:, None]


def centre(field):
    return field[1:-1, 1:-1]


def along_lon(field):
    return 0.5 * (field[1:-1, 2:] - field[1:-1, :-2])


def along_lat(field):
    return 0.5 * (field[2:, 1:-1] - field[:-2, 1:-1])


def tendency(padded, coriolis):
    height = padded[0]
    zonal = padded[1]
    meridional = padded[2]
    depth = 1.0 + height
    height_rate = -(along_lon(depth * zonal) + along_lat(depth * meridional))
    zonal_mid = centre(zonal)
    merid_mid = centre(meridional)
    zonal_rate = (
        -(zonal_mid * along_lon(zonal) + merid_mid * along_lat(zonal))
        + coriolis * merid_mid
        - along_lon(height)
    )
    merid_rate = (
        -(zonal_mid * along_lon(meridional) + merid_mid * along_lat(meridional))
        - coriolis * zonal_mid
        - along_lat(height)
    )
    return jnp.stack([height_rate, zonal_rate, merid_rate])


def margin_rows(coriolis, outer, keep):
    cut_rows = outer - keep
    return coriolis[cut_rows : coriolis.shape[0] - cut_rows]


def fourier_table(length):
    midpoint_split = length // 2
    index = jnp.arange(length, dtype=jnp.int32)
    wave = jnp.where(index <= midpoint_split, index, index - midpoint_split)
    product = index[:, None] * wave[None, :] % length
    angle = 2.0 * jnp.pi / length * product.astype(jnp.float32)
    return jnp.where(index[None, :] <= midpoint_split, jnp.cos(angle), jnp.sin(angle))


def shards(segment_launch_values, initial_backdrop, spectral_inverse_variances):
    flow_variables = segment_launch_values[0]
    lat_rows = flow_variables.shape[1]
    total_lat = lat_rows * lax.axis_size("lat")
    first_row = lax.axis_index("lat") * lat_rows
    outer = 3 * STEPS
    coriolis = latitude_tendencies(total_lat, first_row - outer, lat_rows + 2 * outer)
    state = padded_2(flow_variables, (("lat", 1), ("lon", 2)), outer)
    for step_number in range(STEPS):
        border_rows = outer - 3 * step_number
        first = state[:, 1:-1, 1:-1] + time_step * tendency(
            state, margin_rows(coriolis, outer, border_rows - 1)
        )
        second = 0.75 * state[:, 2:-2, 2:-2] + 0.25 * (
            first[:, 1:-1, 1:-1]
            + time_step * tendency(first, margin_rows(coriolis, outer, border_rows - 2))
        )
        state = 1.0 / 3.0 * state[:, 3:-3, 3:-3] + 2.0 / 3.0 * (
            second[:, 1:-1, 1:-1]
            + time_step * tendency(second, margin_rows(coriolis, outer, border_rows - 3))
        )
    flow_variables = state
    arrived = from_behind(flow_variables, "sub", 1)
    preceding_interval = jnp.where(lax.axis_index("sub") == 0, initial_backdrop, arrived)
    mismatch_misfits = segment_launch_values[0] - preceding_interval
    table = fourier_table(NLON)
    midpoint_split = NLON // 2
    column = jnp.arange(NLON, dtype=jnp.int32)
    factor = (
        jnp.where((column == 0) | (column == midpoint_split), 1.0, 2.0).astype(jnp.float32) / NLON
    )
    weights_full = (
        jnp.concatenate(
            [spectral_inverse_variances, spectral_inverse_variances[:, 1:midpoint_split]], axis=1
        )
        * factor[None, :]
    )
    whole_rows = lax.all_to_all(mismatch_misfits, "lon", split_axis=1, concat_axis=2, tiled=True)
    spectral_coefficients = jnp.einsum(
        "fan,nc->fac", whole_rows, table, precision=lax.Precision.HIGHEST
    )
    restored = jnp.einsum(
        "fac,nc->fan",
        spectral_coefficients * weights_full[:, None, :],
        table,
        precision=lax.Precision.HIGHEST,
    )
    weighted = lax.all_to_all(restored, "lon", split_axis=2, concat_axis=1, tiled=True)
    return weighted[None]


def solution(mesh):
    return jax.shard_map(
        shards,
        mesh=mesh,
        in_specs=(P("sub", None, "lat", "lon"), P(None, "lat", "lon"), P()),
        out_specs=P("sub", None, "lat", "lon"),
        check_vma=False,
    )
```

profile of v0, /device:TPU:1, one launch (start us, length us, event | category | flops | bytes accessed | tf_op | source)
XLA Modules:
  0.0 245.5 jit_solution(14291869343783942433)
XLA Ops:
  0.0 1.9 copy.9
  3.0 2.1 collective-permute-start
  5.1 2.1 copy.11
  7.2 6.8 %collective-permute-done = f32[3,9,256]{1,2,0:T(8,128)S(1)} collective-permute-done((f32[3,9,256]{1,2,0:T(8,128)}, f32[3,9,256]{1,2,0:T(8,128)S(1)}, u32[]{:S(2)}, u32[]{:S(2)}) %collective-permute-start) | collective-permute-done | bytes 27680 | tf_op jit(solution)/shard_map/ppermute | solution.py:20
  14.4 8.2 %collective-permute-done.1 = f32[3,9,256]{1,2,0:T(8,128)S(1)} collective-permute-done((f32[3,9,256]{1,2,0:T(8,128)S(1)}, f32[3,9,256]{1,2,0:T(8,128)S(1)}, u32[]{:S(2)}, u32[]{:S(2)}) %collective-permute-start.1) | collective-permute-done | bytes 27680 | tf_op jit(solution)/shard_map/ppermute | solution.py:23
  24.3 2.1 collective-permute-start.3
  28.8 3.6 %pad_maximum_fusion = f32[3,530,274]{1,0,2:T(4,128)S(1)} fusion(f32[3,530,9]{1,0,2:T(4,128)S(1)} %collective-permute-done.3, f32[3,9,256]{1,0,2:T(4,128)S(1)} %copy.12, f32[3,512,256]{1,0,2:T(4,128)S(1)} %copy.11, f32[3,9,256]{1,0,2:T(4,128)S(1)} %copy.10, f32[3,530,9]{1,0,2:T(4,128)S(1)} %collective-permute-done.2), kind=kLoop, calls=%fused_computation.14 | loop fusion | flops 1742640 | bytes 3485280 | tf_op jit(solution)/shard_map/concatenate | solution.py:24
  36.3 2.1 fusion.109
  41.2 2.1 fusion.85
  44.3 1.7 slice.883
  46.6 2.1 fusion.61
  50.3 2.1 fusion.37
  54.0 2.1 fusion.205
  56.1 2.0 fusion.20
  58.9 2.0 fusion.181
  63.4 2.0 fusion.157
  67.0 2.2 fusion.133
  71.5 1.6 fusion.229
  73.1 2.3 fusion.22
  75.4 5.9 %collective-permute-start.4 = (f32[3,512,256]{1,2,0:T(8,128)}, f32[3,512,256]{1,2,0:T(8,128)}, u32[]{:S(2)}, u32[]{:S(2)}) collective-permute-start(f32[3,512,256]{1,2,0:T(8,128)} %fusion.22), channel_id=1, source_target_pairs={{0,8},{8,16},{16,24},{1,9},{9,17},{17,25},{2,10},{10,18},{18,26},{... | collective-permute-start | bytes 4718600 | tf_op jit(solution)/shard_map/ppermute | solution.py:31
  81.4 1.6 copy.18
  83.0 16.0 %collective-permute-done.4 = f32[3,512,256]{1,2,0:T(8,128)} collective-permute-done((f32[3,512,256]{1,2,0:T(8,128)}, f32[3,512,256]{1,2,0:T(8,128)}, u32[]{:S(2)}, u32[]{:S(2)}) %collective-permute-start.4) | collective-permute-done | bytes 1572896 | tf_op jit(solution)/shard_map/ppermute | solution.py:31
  99.0 2.0 select_subtract_fusion
  101.0 1.8 copy.19
  102.8 4.2 %all-to-all-start = ((f32[3,512,256]{2,0,1:T(4,128)}), f32[3,512,256]{2,0,1:T(4,128)S(1)}, u32[]{:S(2)}, u32[]{:S(2)}) async-start(f32[3,512,256]{2,0,1:T(4,128)} %copy.19), calls=%async_computation | async-start | bytes 4194304 | tf_op jit(solution)/shard_map/all_to_all | solution.py:123
  107.2 33.0 %all-to-all-done = f32[3,512,256]{2,0,1:T(4,128)S(1)} async-done(((f32[3,512,256]{2,0,1:T(4,128)}), f32[3,512,256]{2,0,1:T(4,128)S(1)}, u32[]{:S(2)}, u32[]{:S(2)}) %all-to-all-start) | async-done | bytes 1572896 | tf_op jit(solution)/shard_map/all_to_all | solution.py:123
  141.5 1.9 copy.21
  143.4 27.0 %fusion.5 = f32[3,128,1024]{2,1,0:T(8,128)S(1)} fusion(f32[3,128,1024]{1,2,0:T(8,128)S(1)} %bitcast.203, s32[1024]{0:T(1024)S(1)} %add_select_fusion.1, pred[1024]{0:T(1024)(128)(4,1)S(1)} %iota_compare_fusion.2), kind=kOutput, calls=%fused_computation.8 | convolution fusion | flops 4847566848 | bytes 3150848 | tf_op jit(solution)/shard_map/fan,nc->fac/dot_general | solution.py:124
  170.4 23.2 %fusion.3 = f32[3,128,1024]{2,1,0:T(8,128)} fusion(s32[1024]{0:T(1024)S(1)} %add_select_fusion.1, pred[1024]{0:T(1024)(128)(4,1)S(1)} %iota_compare_fusion.2, f32[3,128,1024]{2,1,0:T(8,128)S(1)} %fusion.5, f32[3,1024]{1,0:T(4,128)S(1)} %maximum_multiply_fusion.9), kind=kOutput, calls=%fused_computation.6 | convolution fusion | flops 4847960064 | bytes 3163136 | tf_op jit(solution)/shard_map/fac,nc->fan/dot_general | solution.py:127
  193.6 1.9 copy.23
  195.6 47.0 %all_to_all.33 = f32[3,128,1024]{1,0,2:T(4,128)} all-to-all(f32[3,128,1024]{1,0,2:T(4,128)S(1)} %copy.23), channel_id=1, replica_groups=mesh['sub'=4,'lat'=2,'lon'=4] {'lon'}, dimensions={2} | all-to-all | bytes 3145728 | tf_op jit(solution)/shard_map/all_to_all | solution.py:133
  242.5 2.7 %copy.24 = f32[3,4,128,256]{3,2,1,0:T(8,128)} copy(f32[3,4,128,256]{2,0,3,1:T(4,128)} %bitcast.200) | data formatting | bytes 3145728 | tf_op jit(solution)/shard_map/all_to_all | solution.py:133
  (70 shorter events, 25.6 us)
Async XLA Ops:
  1.9 3.2 %copy-start = (f32[1,3,512,256]{2,3,1,0:T(8,128)}, f32[1,3,512,256]{2,3,1,0:T(8,128)S(1)}, u32[]{:S(2)}) copy-start(f32[1,3,512,256]{2,3,1,0:T(8,128)S(1)} %copy.9) | copy-start | bytes 4718596
  3.0 11.1 %collective-permute-start = (f32[3,9,256]{1,2,0:T(8,128)}, f32[3,9,256]{1,2,0:T(8,128)S(1)}, u32[]{:S(2)}, u32[]{:S(2)}) collective-permute-start(f32[3,9,256]{1,2,0:T(8,128)} %get-tuple-element.68), channel_id=1, source_target_pairs={{0,4},{4,0},{1,5},{5,1},{2,6},{6,2},{3,7},{7,3},{8,12},{12,8},{9,1... | collective-permute-start | bytes 82952 | tf_op jit(solution)/shard_map/ppermute | solution.py:20
  5.1 17.5 %collective-permute-start.1 = (f32[3,9,256]{1,2,0:T(8,128)S(1)}, f32[3,9,256]{1,2,0:T(8,128)S(1)}, u32[]{:S(2)}, u32[]{:S(2)}) collective-permute-start(f32[3,9,256]{1,2,0:T(8,128)S(1)} %get-tuple-element.69), channel_id=1, source_target_pairs={{4,0},{0,4},{5,1},{1,5},{6,2},{2,6},{7,3},{3,7},{12,8},{8,12},{13,... | collective-permute-start | bytes 82952 | tf_op jit(solution)/shard_map/ppermute | solution.py:23
  23.0 5.4 %collective-permute-start.2 = (f32[3,530,9]{1,0,2:T(4,128)S(1)}, f32[3,530,9]{1,0,2:T(4,128)S(1)}, u32[]{:S(2)}, u32[]{:S(2)}) collective-permute-start(f32[3,530,9]{1,0,2:T(4,128)S(1)} %get-tuple-element.5), channel_id=1, source_target_pairs={{0,1},{1,2},{2,3},{3,0},{4,5},{5,6},{6,7},{7,4},{8,9},{9,10},{10,1... | collective-permute-start | bytes 171728 | tf_op jit(solution)/shard_map/ppermute | solution.py:20
  24.3 4.6 %collective-permute-start.3 = (f32[3,530,9]{1,0,2:T(4,128)S(1)}, f32[3,530,9]{1,0,2:T(4,128)S(1)}, u32[]{:S(2)}, u32[]{:S(2)}) collective-permute-start(f32[3,530,9]{1,0,2:T(4,128)S(1)} %get-tuple-element.6), channel_id=1, source_target_pairs={{1,0},{2,1},{3,2},{0,3},{5,4},{6,5},{7,6},{4,7},{9,8},{10,9},{11,1... | collective-permute-start | bytes 171728 | tf_op jit(solution)/shard_map/ppermute | solution.py:23
  73.1 8.2 %copy-start.2 = (f32[3,512,256]{2,1,0:T(8,128)S(1)}, f32[3,512,256]{2,1,0:T(8,128)}, u32[]{:S(2)}) copy-start(f32[3,512,256]{2,1,0:T(8,128)} %param.4) | copy-start | bytes 4718596
  75.4 23.6 %copy-start.1 = (f32[1,3,512,256]{2,3,1,0:T(8,128)S(1)}, f32[1,3,512,256]{2,3,1,0:T(8,128)}, u32[]{:S(2)}) copy-start(f32[1,3,512,256]{2,3,1,0:T(8,128)} %copy-done) | copy-start | bytes 4718596
  75.4 23.6 %collective-permute-start.4 = (f32[3,512,256]{1,2,0:T(8,128)}, f32[3,512,256]{1,2,0:T(8,128)}, u32[]{:S(2)}, u32[]{:S(2)}) collective-permute-start(f32[3,512,256]{1,2,0:T(8,128)} %fusion.22), channel_id=1, source_target_pairs={{0,8},{8,16},{16,24},{1,9},{9,17},{17,25},{2,10},{10,18},{18,26},{... | collective-permute-start | bytes 4718600 | tf_op jit(solution)/shard_map/ppermute | solution.py:31
  102.8 4.2 %copy-start.3 = (f32[3,513]{1,0:T(4,128)S(1)}, f32[3,513]{1,0:T(4,128)}, u32[]{:S(2)}) copy-start(f32[3,513]{1,0:T(4,128)} %param.5) | copy-start | bytes 18472
  102.8 37.3 %all-to-all-start = ((f32[3,512,256]{2,0,1:T(4,128)}), f32[3,512,256]{2,0,1:T(4,128)S(1)}, u32[]{:S(2)}, u32[]{:S(2)}) async-start(f32[3,512,256]{2,0,1:T(4,128)} %copy.19), calls=%async_computation | async-start | bytes 4194304 | tf_op jit(solution)/shard_map/all_to_all | solution.py:123
where the time goes:
time: 249 us; the launch traced here: 245 us
  waiting for transfers between devices  65.8 us (26%)
  matrix products  50.2 us (20%)
  blocking collectives  47 us (19%)
  other arithmetic  41.3 us (17%)
  local copies, waits for them, and re-layouts  25.1 us (10%)
  starting transfers between devices  15.5 us (6%)
    all_to_all x1, blocking collectives, shards(): lax.all_to_all(restored, 'lon', split_axis=2, concat_axis=1, tiled=True)  47 us
    all_to_all x1, waiting for transfers between devices, shards(): lax.all_to_all(mismatch_misfits, 'lon', split_axis=1, concat_axis=2, tile...  33 us
    dot_general x1, matrix products, shards(): jnp.einsum('fan,nc->fac', whole_rows, table, precision=lax.Precision.HIGH...  27 us
    another operation x18, other arithmetic, tendency(): return jnp.stack([height_rate, zonal_rate, merid_rate])  24 us
    dot_general x1, matrix products, shards(): jnp.einsum('fac,nc->fan', spectral_coefficients * weights_full[:, None, :...  23.2 us
    ppermute x1, waiting for transfers between devices, from_behind(): lax.ppermute(value, axis, [(source, source + steps) for source in range(f...  16 us
    ppermute x2, waiting for transfers between devices, padded_2(): lax.ppermute(lax.slice_in_dim(block, 0, width, axis=dim), axis, backward)  8.66 us
    ppermute x2, waiting for transfers between devices, padded_2(): lax.ppermute(lax.slice_in_dim(block, block.shape[dim] - width, None, axis...  8.12 us
  transfers between devices with their start and end apart: 6, of which 6 were waited for; matrix products, arithmetic and copies ran while one was open for 2% of the time, Pallas kernels for 0%

commit v1 on v0

v1 whole, which is shorter than its diff:
```python
import numpy as np
import jax
import jax.numpy as jnp
from jax import lax
from jax.experimental import pallas as pl
from jax.experimental.pallas import tpu as pltpu
from jax.sharding import PartitionSpec as P

STEPS = 3
HALO = 16
BLOCK = 4
MESH = pl.DeviceIdType.MESH

time_step = 0.5
coriolis_peak = 0.4


def cosine_table(length):
    half = length // 2
    wave = np.arange(half)[:, None]
    angle = (wave * np.arange(length)[None, :]) % length * (2.0 * np.pi / length)
    return (np.where(wave == 0, 1.0, 2.0) / length * np.cos(angle)).astype(np.float32)


def doubled_coriolis(total_rows):
    index = np.arange(total_rows)
    return (2.0 * coriolis_peak * np.sin(2.0 * np.pi * (index + 0.5) / total_rows)).astype(
        np.float32
    )


def split_parts(value):
    high = value.astype(jnp.bfloat16)
    return high, (value - high.astype(jnp.float32)).astype(jnp.bfloat16)


def kernel(
    nsub, nlat, nlon, x_hbm, back_hbm, w_ref, table_hbm, f_smem, out_ref,
    table, wpad, wave_row, conv_hi, conv_lo, frows, slab, fc, state, mid1, mid2,
    y_own, y_next, got_own, got_next,
    table_sem, main_send, top_send, bot_send, main_recv, top_recv, bot_recv,
    back_send, back_recv, own_send, own_recv, next_send, next_recv,
):
    k = lax.axis_index("sub")
    a = lax.axis_index("lat")
    z = lax.axis_index("lon")
    fields, lat_rows, width = x_hbm.shape
    rows = lat_rows // nlon
    total = lat_rows * nlat
    length = width * nlon
    half = length // 2
    lanes = 128
    slices = length // lanes
    padded = rows + 2 * HALO
    k_up = lax.rem(k + 1, nsub)
    k_down = lax.rem(k + nsub - 1, nsub)
    a_up = lax.rem(a + 1, nlat)
    a_down = lax.rem(a + nlat - 1, nlat)
    last = nsub - 1

    barrier = pltpu.get_barrier_semaphore()
    for d in range(1, nlon):
        pl.semaphore_signal(
            barrier, inc=1, device_id=(k, a, lax.rem(z + d, nlon)), device_id_type=MESH
        )
    for d in range(nlon):
        for there in ((k, a_up), (k, a_down), (k_up, a), (k_down, a)):
            pl.semaphore_signal(barrier, inc=1, device_id=there + (jnp.int32(d),), device_id_type=MESH)
    pl.semaphore_wait(barrier, nlon - 1 + 4 * nlon)

    mine = pl.ds(pl.multiple_of(z * width, width), width)

    def local(src, dst, sem):
        return pltpu.make_async_copy(src, dst, sem)

    def remote(src, dst, send, recv, there):
        return pltpu.make_async_remote_copy(
            src_ref=src, dst_ref=dst, send_sem=send, recv_sem=recv,
            device_id=there, device_id_type=MESH,
        )

    def rows_at(first, count):
        return pl.ds(pl.multiple_of(first, 8), count)

    def edge(target, up):
        if up:
            src = x_hbm.at[:, pl.ds(target * rows + rows - HALO, HALO), :]
            dst = slab.at[:, pl.ds(0, HALO), mine]
            lon, lat = (target + 1) % nlon, a_up if target == nlon - 1 else a
            send, recv = top_send.at[target], top_recv.at[z]
        else:
            src = x_hbm.at[:, pl.ds(target * rows, HALO), :]
            dst = slab.at[:, pl.ds(HALO + rows, HALO), mine]
            lon, lat = (target - 1) % nlon, a_down if target == 0 else a
            send, recv = bot_send.at[target], bot_recv.at[z]
        crosses = target == (nlon - 1 if up else 0)
        return src, dst, send, recv, lon, lat, crosses

    def exchange(src_hbm, dst, sends, recvs, first):
        def copy_of(d):
            zt = lax.rem(z + d, nlon)
            src = src_hbm.at[:, rows_at(zt * rows, rows), :]
            into = dst.at[:, pl.ds(first, rows), mine]
            if d == 0:
                return local(src, into, recvs.at[z])
            return remote(src, into, sends.at[d], recvs.at[z], (k, a, zt))

        return [copy_of(d) for d in range(nlon)]

    mains = exchange(x_hbm, slab, main_send, main_recv, HALO)
    for d in (1, nlon - 1) if nlon > 2 else (1,):
        mains[d].start()
    for d in range(2, nlon - 1):
        mains[d].start()
    mains[0].start()
    for up in (True, False):
        for target in range(nlon):
            src, dst, send, recv, lon, lat, crosses = edge(target, up)
            if crosses:
                remote(src, dst, send, recv, (k, lat, jnp.int32(lon))).start()
            else:
                @pl.when(z == lon)
                def _():
                    local(src, dst, recv).start()

                @pl.when(z != lon)
                def _():
                    remote(src, dst, send, recv, (k, lat, jnp.int32(lon))).start()

    table_copy = local(table_hbm, table, table_sem)
    table_copy.start()
    wpad[...] = jnp.zeros_like(wpad)
    wpad[0:fields, 0 : half + 1] = w_ref[...]
    table_copy.wait()
    sign = 1.0 - 2.0 * (lax.broadcasted_iota(jnp.int32, (8, length), 1) % 2).astype(jnp.float32)
    wave_row[...] = (
        jnp.dot(
            wpad[:, 0:half], table[...], precision=lax.Precision.HIGHEST,
            preferred_element_type=jnp.float32,
        )
        + wpad[:, half : half + 1] * (sign / length)
    )
    chunk = 16
    blocks = half // lanes
    for c in range(fields):
        line = 0.5 * wave_row[c : c + 1, :]

        @pl.loop(0, lanes // chunk)
        def _(i):
            row = i * chunk + lax.broadcasted_iota(jnp.int32, (chunk, length), 0)
            turned = jnp.broadcast_to(line, (chunk, length))
            for bit in range(lanes.bit_length() - 1):
                far = pltpu.roll(turned, 1 << bit, 1)
                turned = jnp.where((row >> bit) % 2 == 1, far, turned)
            for q in range(slices):
                first = turned[:, q * lanes : (q + 1) * lanes]
                p = (q + blocks) % slices
                other = turned[:, p * lanes : (p + 1) * lanes]
                for part, value in enumerate((first + other, first - other)):
                    high, low = split_parts(value)
                    for m in range(blocks):
                        t = (q + m) % slices
                        if t < blocks:
                            at = pl.ds(pl.multiple_of(m * lanes + i * chunk, chunk), chunk)
                            conv_hi[2 * c + part, at, t * lanes : (t + 1) * lanes] = high
                            conv_lo[2 * c + part, at, t * lanes : (t + 1) * lanes] = low

    first_row = (a * nlon + z) * rows - HALO + total

    @pl.loop(0, padded)
    def _(r):
        frows[pl.ds(pl.multiple_of(8 * r, 8), 8), :] = jnp.full(
            (8, lanes), f_smem[lax.rem(first_row + r, total)], jnp.float32
        )

    for s in range(nlon):
        cols = pl.ds(s * width, width)
        for first, count, recv in (
            (HALO, rows, main_recv), (0, HALO, top_recv), (HALO + rows, HALO, bot_recv)
        ):
            block = slab.at[:, pl.ds(first, count), cols]
            local(block, block, recv.at[s]).wait()

    backs = exchange(back_hbm, fc, back_send, back_recv, 0)

    @pl.when(k == last)
    def _():
        for d in range(nlon):
            backs[d].start()

    def filtered(source, first, c):
        value = source[c, pl.ds(first, rows), :]
        left, right = value[:, :half], value[:, half:]
        halves = []
        for part, mix in enumerate((left + right, left - right)):
            high, low = split_parts(mix)
            both = jnp.concatenate([high, low], axis=0)
            twice = jnp.dot(both, conv_hi[2 * c + part], preferred_element_type=jnp.float32)
            rest = jnp.dot(high, conv_lo[2 * c + part], preferred_element_type=jnp.float32)
            halves.append(twice[:rows] + (twice[rows:] + rest))
        return halves[0] + halves[1], halves[0] - halves[1]

    def home(c, d, y, got, sends, recvs, sub, own):
        zt = lax.rem(z + d, nlon)
        src = y.at[c, :, pl.ds(pl.multiple_of(zt * width, width), width)]
        dst = got.at[c, rows_at(z * rows, rows), :]
        if own and d == 0:
            return local(src, dst, recvs.at[c, z])
        return remote(src, dst, sends.at[c, d], recvs.at[c, z], (sub, a, zt))

    order = [d for d in (1, nlon - 1) if d > 0]
    order = list(dict.fromkeys(order)) + [d for d in range(2, nlon - 1)] + [0]

    def filter_and_send(source, first, y, got, sends, recvs, sub, own):
        @pl.loop(0, fields)
        def _(c):
            low, high = filtered(source, first, c)
            y[c, :, 0:half] = low
            y[c, :, half:length] = high
            for d in order:
                home(c, d, y, got, sends, recvs, sub, own).start()

    filter_and_send(slab, HALO, y_own, got_own, own_send, own_recv, k, True)

    @pl.when(k < last)
    def _():
        group = 32

        @pl.loop(0, padded // group)
        def _(i):
            r0 = pl.multiple_of(i * group, group)
            for c in range(fields):
                for s in range(slices):
                    state[c, pl.ds(8 * r0 + s, group, stride=8), :] = slab[
                        c, pl.ds(r0, group), s * lanes : (s + 1) * lanes
                    ]

        lane = lax.broadcasted_iota(jnp.int32, (BLOCK, 8, lanes), 2)
        at_first, at_last = lane == 0, lane == lanes - 1

        def across(v):
            ahead = pltpu.roll(jnp.where(at_first, pltpu.roll(v, 7, 1), v), lanes - 1, 2)
            behind = pltpu.roll(jnp.where(at_last, pltpu.roll(v, 1, 1), v), 1, 2)
            return ahead - behind

        def stage(arg, base, out, keep, mix, gain):
            @pl.loop(0, (padded - HALO) // BLOCK)
            def _(i):
                r0 = 8 + i * BLOCK
                wide = pl.ds(pl.multiple_of(8 * (r0 - 1), 8), 8 * (BLOCK + 2))
                at = pl.ds(pl.multiple_of(8 * r0, 8), 8 * BLOCK)
                h, u, v = [arg[c, wide, :].reshape(BLOCK + 2, 8, lanes) for c in range(3)]
                f2 = frows[at, :].reshape(BLOCK, 8, lanes)
                hm, um, vm = [q[1:-1] for q in (h, u, v)]

                def along(q):
                    return q[2:] - q[:-2]

                dv = v + h * v
                rate_h = across(um + hm * um) + along(dv)
                rate_u = um * across(um) + vm * along(u) + across(hm) - f2 * vm
                rate_v = um * across(vm) + vm * along(v) + along(h) + f2 * um
                for c, (m, rate) in enumerate(((hm, rate_h), (um, rate_u), (vm, rate_v))):
                    if base is None:
                        value = m - gain * rate
                    else:
                        old = base[c, at, :].reshape(BLOCK, 8, lanes)
                        value = keep * old + mix * m - gain * rate
                    out[c, at, :] = value.reshape(8 * BLOCK, lanes)

        half_step = 0.5 * time_step

        @pl.loop(0, STEPS)
        def _(step):
            stage(state, None, mid1, 0.0, 1.0, half_step)
            stage(mid1, state, mid2, 0.75, 0.25, 0.25 * half_step)
            stage(mid2, state, state, 1.0 / 3.0, 2.0 / 3.0, 2.0 / 3.0 * half_step)

        @pl.loop(0, rows // group)
        def _(i):
            r0 = pl.multiple_of(i * group, group)
            for c in range(fields):
                for s in range(slices):
                    fc[c, pl.ds(r0, group), s * lanes : (s + 1) * lanes] = state[
                        c, pl.ds(8 * (r0 + HALO) + s, group, stride=8), :
                    ]

    @pl.when(k == last)
    def _():
        for s in range(nlon):
            block = fc.at[:, :, pl.ds(s * width, width)]
            local(block, block, back_recv.at[s]).wait()
        for d in range(1, nlon):
            backs[d].wait_send()

    filter_and_send(fc, 0, y_next, got_next, next_send, next_recv, k_up, False)

    for c in range(fields):
        for s in range(nlon):
            for got, recvs in ((got_own, own_recv), (got_next, next_recv)):
                block = got.at[c, pl.ds(s * rows, rows), :]
                local(block, block, recvs.at[c, s]).wait()
            part = pl.ds(s * rows, rows)
            out_ref[c, part, :] = got_own[c, part, :] - got_next[c, part, :]

    for d in range(1, nlon):
        mains[d].wait_send()
    for up in (True, False):
        for target in range(nlon):
            src, dst, send, recv, lon, lat, crosses = edge(target, up)
            if crosses:
                remote(src, dst, send, recv, (k, lat, jnp.int32(lon))).wait_send()
            else:
                @pl.when(z != lon)
                def _():
                    remote(src, dst, send, recv, (k, lat, jnp.int32(lon))).wait_send()
    for c in range(fields):
        for d in range(nlon):
            if d:
                home(c, d, y_own, got_own, own_send, own_recv, k, True).wait_send()
            home(c, d, y_next, got_next, next_send, next_recv, k_up, False).wait_send()


def solution(mesh):
    nsub, nlat, nlon = mesh.shape["sub"], mesh.shape["lat"], mesh.shape["lon"]

    def shards(launch, backdrop, inverse_variances):
        tile = launch[0]
        fields, lat_rows, width = tile.shape
        length = width * nlon
        half = length // 2
        rows = lat_rows // nlon
        padded = rows + 2 * HALO
        f32, bf16 = jnp.float32, jnp.bfloat16
        dma = pltpu.SemaphoreType.DMA
        any_space = pl.BlockSpec(memory_space=pl.ANY)
        vmem = pl.BlockSpec(memory_space=pltpu.VMEM)
        rows_like = pltpu.VMEM((fields, padded * 8, 128), f32)
        tile_like = pltpu.VMEM((fields, lat_rows, width), f32)
        slab_like = pltpu.VMEM((fields, rows, length), f32)
        out = pl.pallas_call(
            lambda *refs: kernel(nsub, nlat, nlon, *refs),
            name="weighted_defects",
            out_shape=jax.ShapeDtypeStruct(tile.shape, f32),
            in_specs=[any_space, any_space, vmem, any_space,
                      pl.BlockSpec(memory_space=pltpu.SMEM)],
            out_specs=vmem,
            scratch_shapes=[
                pltpu.VMEM((half, length), f32),
                pltpu.VMEM((8, half + 128), f32),
                pltpu.VMEM((8, length), f32),
                pltpu.VMEM((2 * fields, half, half), bf16),
                pltpu.VMEM((2 * fields, half, half), bf16),
                pltpu.VMEM((padded * 8, 128), f32),
                pltpu.VMEM((fields, padded, length), f32),
                slab_like,
                rows_like, rows_like, rows_like,
                slab_like, slab_like, tile_like, tile_like,
                dma,
                dma((nlon,)), dma((nlon,)), dma((nlon,)),
                dma((nlon,)), dma((nlon,)), dma((nlon,)),
                dma((nlon,)), dma((nlon,)),
                dma((fields, nlon)), dma((fields, nlon)),
                dma((fields, nlon)), dma((fields, nlon)),
            ],
            compiler_params=pltpu.CompilerParams(collective_id=0, has_side_effects=True),
        )(
            tile, backdrop, inverse_variances,
            jnp.asarray(cosine_table(length)), jnp.asarray(doubled_coriolis(lat_rows * nlat)),
        )
        return out[None]

    return jax.shard_map(
        shards,
        mesh=mesh,
        in_specs=(P("sub", None, "lat", "lon"), P(None, "lat", "lon"), P()),
        out_specs=P("sub", None, "lat", "lon"),
        check_vma=False,
    )
```

time: 249 us -> 142 us (0.57)
  the two profiles are of different devices: /device:TPU:1 before, /device:TPU:0 now
where the time goes in v1:
time: 142 us; the launch traced here: 141 us
  Pallas kernels  139 us (98%)
  local copies, waits for them, and re-layouts  2.65 us (2%)
    pallas_call x1, Pallas kernels, shards(): pl.pallas_call(lambda *refs: kernel(nsub, nlat, nlon, *refs), name='weigh...  139 us

profile of v1, /device:TPU:0, one launch (start us, length us, event | category | flops | bytes accessed | tf_op | source)
XLA Modules:
  0.0 141.4 jit_solution(6705818489199319214)
XLA Ops:
  0.0 138.7 %weighted_defects.1 = f32[3,512,256]{2,1,0:T(8,128)} custom-call(f32[3,512,256]{2,1,0:T(8,128)} %bitcast.3, f32[3,512,256]{2,1,0:T(8,128)} %refs_1_.1, f32[3,513]{1,0:T(4,128)} %refs_2_.1, f32[512,1024]{1,0:T(8,128)} %constant.4.clone.refs_3_, f32[1024]{0:T(1024)} %constant.5.clone.refs_4_), custom_call_target="tpu_custom_call" | custom-call | tf_op jit(solution)/shard_map/weighted_defects/pallas_call | solution.py:341
  138.7 2.7 %copy.7 = f32[1,3,512,256]{3,2,1,0:T(8,128)} copy(f32[1,3,512,256]{3,2,1,0:T(8,128)} %bitcast.2) | data formatting | bytes 3145728

commit v2 on v1

--- a/solution.py
+++ b/solution.py
@@ -37,9 +37,9 @@
 def kernel(
     nsub, nlat, nlon, x_hbm, back_hbm, w_ref, table_hbm, f_smem, out_ref,
     table, wpad, wave_row, conv_hi, conv_lo, frows, slab, fc, state, mid1, mid2,
-    y_own, y_next, got_own, got_next,
+    prev, y_own, got_own,
     table_sem, main_send, top_send, bot_send, main_recv, top_recv, bot_recv,
-    back_send, back_recv, own_send, own_recv, next_send, next_recv,
+    back_send, back_recv, own_send, own_recv, hop_send, hop_recv,
 ):
     k = lax.axis_index("sub")
     a = lax.axis_index("lat")
@@ -188,8 +188,8 @@
         for d in range(nlon):
             backs[d].start()
 
-    def filtered(source, first, c):
-        value = source[c, pl.ds(first, rows), :]
+    def filtered(c):
+        value = slab[c, pl.ds(HALO, rows), :] - prev[c]
         left, right = value[:, :half], value[:, half:]
         halves = []
         for part, mix in enumerate((left + right, left - right)):
@@ -200,27 +200,19 @@
             halves.append(twice[:rows] + (twice[rows:] + rest))
         return halves[0] + halves[1], halves[0] - halves[1]
 
-    def home(c, d, y, got, sends, recvs, sub, own):
+    def home(c, d):
         zt = lax.rem(z + d, nlon)
-        src = y.at[c, :, pl.ds(pl.multiple_of(zt * width, width), width)]
-        dst = got.at[c, rows_at(z * rows, rows), :]
-        if own and d == 0:
-            return local(src, dst, recvs.at[c, z])
-        return remote(src, dst, sends.at[c, d], recvs.at[c, z], (sub, a, zt))
+        src = y_own.at[c, :, pl.ds(pl.multiple_of(zt * width, width), width)]
+        dst = got_own.at[c, rows_at(z * rows, rows), :]
+        if d == 0:
+            return local(src, dst, own_recv.at[c, z])
+        return remote(src, dst, own_send.at[c, d], own_recv.at[c, z], (k, a, zt))
+
+    def hop(c):
+        return remote(fc.at[c], prev.at[c], hop_send.at[c], hop_recv.at[c], (k_up, a, z))
 
     order = [d for d in (1, nlon - 1) if d > 0]
     order = list(dict.fromkeys(order)) + [d for d in range(2, nlon - 1)] + [0]
-
-    def filter_and_send(source, first, y, got, sends, recvs, sub, own):
-        @pl.loop(0, fields)
-        def _(c):
-            low, high = filtered(source, first, c)
-            y[c, :, 0:half] = low
-            y[c, :, half:length] = high
-            for d in order:
-                home(c, d, y, got, sends, recvs, sub, own).start()
-
-    filter_and_send(slab, HALO, y_own, got_own, own_send, own_recv, k, True)
 
     @pl.when(k < last)
     def _():
@@ -293,15 +285,24 @@
         for d in range(1, nlon):
             backs[d].wait_send()
 
-    filter_and_send(fc, 0, y_next, got_next, next_send, next_recv, k_up, False)
+    for c in range(fields):
+        hop(c).start()
+
+    @pl.loop(0, fields)
+    def _(c):
+        hop(c).wait_recv()
+        low, high = filtered(c)
+        y_own[c, :, 0:half] = low
+        y_own[c, :, half:length] = high
+        for d in order:
+            home(c, d).start()
 
     for c in range(fields):
         for s in range(nlon):
-            for got, recvs in ((got_own, own_recv), (got_next, next_recv)):
-                block = got.at[c, pl.ds(s * rows, rows), :]
-                local(block, block, recvs.at[c, s]).wait()
             part = pl.ds(s * rows, rows)
-            out_ref[c, part, :] = got_own[c, part, :] - got_next[c, part, :]
+            block = got_own.at[c, part, :]
+            local(block, block, own_recv.at[c, s]).wait()
+            out_ref[c, part, :] = got_own[c, part, :]
 
     for d in range(1, nlon):
         mains[d].wait_send()
@@ -317,8 +318,8 @@
     for c in range(fields):
         for d in range(nlon):
             if d:
-                home(c, d, y_own, got_own, own_send, own_recv, k, True).wait_send()
-            home(c, d, y_next, got_next, next_send, next_recv, k_up, False).wait_send()
+                home(c, d).wait_send()
+        hop(c).wait_send()
 
 
 def solution(mesh):
@@ -355,13 +356,13 @@
                 pltpu.VMEM((fields, padded, length), f32),
                 slab_like,
                 rows_like, rows_like, rows_like,
-                slab_like, slab_like, tile_like, tile_like,
+                slab_like, slab_like, tile_like,
                 dma,
                 dma((nlon,)), dma((nlon,)), dma((nlon,)),
                 dma((nlon,)), dma((nlon,)), dma((nlon,)),
                 dma((nlon,)), dma((nlon,)),
                 dma((fields, nlon)), dma((fields, nlon)),
-                dma((fields, nlon)), dma((fields, nlon)),
+                dma((fields,)), dma((fields,)),
             ],
             compiler_params=pltpu.CompilerParams(collective_id=0, has_side_effects=True),
         )(

time: 142 us -> 127 us (0.89)
  the two profiles are of different devices: /device:TPU:0 before, /device:TPU:1 now
where the time goes in v2:
time: 127 us
  Pallas kernels  124 us (98%)
  local copies, waits for them, and re-layouts  2.65 us (2%)
    pallas_call x1, Pallas kernels, shards(): pl.pallas_call(lambda *refs: kernel(nsub, nlat, nlon, *refs), name='weigh...  124 us
    unnamed x1, local copies, waits for them, and re-layouts  2.65 us

profile of v2, /device:TPU:1, one launch (start us, length us, event | category | flops | bytes accessed | tf_op | source)
XLA Modules:
  0.0 126.9 jit_solution(4833868446642907995)
XLA Ops:
  0.0 124.2 %weighted_defects.1 = f32[3,512,256]{2,1,0:T(8,128)} custom-call(f32[3,512,256]{2,1,0:T(8,128)} %bitcast.3, f32[3,512,256]{2,1,0:T(8,128)} %refs_1_.1, f32[3,513]{1,0:T(4,128)} %refs_2_.1, f32[512,1024]{1,0:T(8,128)} %constant.4.clone.refs_3_, f32[1024]{0:T(1024)} %constant.5.clone.refs_4_), custom_call_target="tpu_custom_call" | custom-call | tf_op jit(solution)/shard_map/weighted_defects/pallas_call | solution.py:342
  124.2 2.7 %copy.7 = f32[1,3,512,256]{3,2,1,0:T(8,128)} copy(f32[1,3,512,256]{3,2,1,0:T(8,128)} %bitcast.2) | data formatting | bytes 3145728
